TPU v7x, 32 devices: a whole 2x2x4 slice. The times are simulated.
32 devices in a mesh: grp: 2 (over core), dev: 16 (over z, y, x).
Axes of the slice: x: 2, y: 2, z: 4, core: 2. Of those that a mesh axis runs over, the one named last changes fastest.
Arguments:
- pixel_tiles: float32 [2048, 6, 512], P(('grp', 'dev')), may hold values from -31 to 31
- blend_source: int32 [2048, 2], P(('grp', 'dev')), may hold values from 0 to 15, all different within a row; in each aligned block of 64 rows (0 to 63, 64 to 127, ...) at most 8 rows name the same one
- blend_slot: int32 [2048, 2], P(('grp', 'dev')), may hold values from 0 to 63
- component_count: int32 [2048], P(('grp', 'dev')), may hold values from 12 to 24
- sed_start: bfloat16 [2048, 24, 6], P(('grp', 'dev')), may hold values from 0.049804688 to 0.5
- morph_start: bfloat16 [2048, 2, 24, 512], P(('grp', 'dev')), may hold values from 0.019897461 to 0.5
Outputs:
- whitened: float32 [2048, 6, 512], P(('grp', 'dev'))
- sed_final: bfloat16 [2048, 24, 6], P(('grp', 'dev'))
Inputs may be any that keep to these rules, and one draw needn't show every extreme that they name: `blend_source`: each blend names 2 different devices of its region; over the blends of one device no device is named more than 8 times, and some device is named exactly 8 times. `blend_slot`: several blends may name the same tile.
All inputs are finite; a program needn't handle non-finite values.
Results may differ from a plain program's by a relative error of at most 0.0052.
Values may be sent and summed in bfloat16 or wider, within the bound.
A program may use at most 64 MiB of HBM per device.

v0:
```python
import math

import jax
import jax.numpy as jnp
from jax import lax
from jax.sharding import PartitionSpec as P

ITERS = 2


def fit_block(blend_data, sed, morph, count):
    components = sed.shape[1]
    active = (jnp.arange(components, dtype=jnp.int32)[None, :] < count[:, None]).astype(jnp.float32)
    sed = (sed.astype(jnp.float32) * active[:, :, None]).astype(jnp.bfloat16)
    morph = morph * active[:, None, :, None].astype(jnp.bfloat16)
    target = blend_data.astype(jnp.float32)
    for sweep in range(ITERS):
        model = jnp.einsum("nkb,nfkp->nfbp", sed, morph, preferred_element_type=jnp.float32)
        misfit = (model - target).astype(jnp.bfloat16)
        gram_matrix = jnp.einsum("nfkp,nfjp->nkj", morph, morph, preferred_element_type=jnp.float32)
        lip_sed = jnp.sqrt(jnp.sum(gram_matrix * gram_matrix, axis=(1, 2))) + 1.0
        gradient = jnp.einsum("nfkp,nfbp->nkb", morph, misfit, preferred_element_type=jnp.float32)
        sed = (
            jnp.maximum(sed.astype(jnp.float32) - gradient / lip_sed[:, None, None], 0.0)
            * active[:, :, None]
        ).astype(jnp.bfloat16)
        model = jnp.einsum("nkb,nfkp->nfbp", sed, morph, preferred_element_type=jnp.float32)
        misfit = (model - target).astype(jnp.bfloat16)
        sed_gram = jnp.einsum("nkb,nkc->nbc", sed, sed, preferred_element_type=jnp.float32)
        lip_morph = jnp.sqrt(jnp.sum(sed_gram * sed_gram, axis=(1, 2))) + 1.0
        grad_morph = jnp.einsum("nkb,nfbp->nfkp", sed, misfit, preferred_element_type=jnp.float32)
        morph = (
            jnp.maximum(morph - (grad_morph + 0.1) / lip_morph[:, None, None, None], 0.0)
            * active[:, None, :, None]
        ).astype(jnp.bfloat16)
    model_out = jnp.einsum("nkb,nfkp->nfbp", sed, morph, preferred_element_type=jnp.float32).astype(
        jnp.bfloat16
    )
    return (sed, morph, model_out)


def on_device(pixel_tiles, blend_source, blend_slot, component_count, sed_start, morph_start):
    peer_count = lax.axis_size("dev")
    blend_rows, footprint = blend_source.shape
    entries = blend_rows * footprint
    capacity = max(2, (entries + peer_count - 1) // peer_count)
    tile_rows, bands, pixels = pixel_tiles.shape
    sources = blend_source.reshape(entries)
    one_hot = (sources[:, None] == jnp.arange(peer_count, dtype=jnp.int32)[None, :]).astype(
        jnp.int32
    )
    ranking = jnp.sum((jnp.cumsum(one_hot, axis=0) - 1) * one_hot, axis=1)
    placing = sources * capacity + ranking
    asking = (
        jnp.zeros((peer_count * capacity,), jnp.int32)
        .at[placing]
        .set(blend_slot.reshape(entries) + 1)
    )
    wanted = lax.all_to_all(
        asking.reshape(peer_count, capacity), "dev", split_axis=0, concat_axis=0, tiled=True
    )
    source_rows = jnp.maximum(wanted - 1, 0).reshape(-1)
    filled = (wanted > 0).reshape(-1)
    outgoing = jnp.where(filled[:, None, None], pixel_tiles[source_rows], 0.0).astype(jnp.bfloat16)
    arrived = lax.all_to_all(
        outgoing.reshape(peer_count, capacity, bands, pixels),
        "dev",
        split_axis=0,
        concat_axis=0,
        tiled=True,
    )
    blend_data = arrived.reshape(peer_count * capacity, bands, pixels)[placing].reshape(
        blend_rows, footprint, bands, pixels
    )
    block_size = math.gcd(blend_rows, 8)
    groups = blend_rows // block_size

    def in_blocks(array):
        return array.reshape((groups, block_size) + array.shape[1:])

    sed_blocks, morph_blocks, model_blocks = lax.map(
        lambda inputs: fit_block(*inputs),
        (
            in_blocks(blend_data),
            in_blocks(sed_start),
            in_blocks(morph_start),
            in_blocks(component_count),
        ),
    )
    sed_final = sed_blocks.reshape(sed_start.shape)
    models = model_blocks.reshape(entries, bands, pixels)
    outbound = (
        jnp.zeros((peer_count * capacity, bands, pixels), jnp.bfloat16).at[placing].set(models)
    )
    returned = lax.all_to_all(
        outbound.reshape(peer_count, capacity, bands, pixels),
        "dev",
        split_axis=0,
        concat_axis=0,
        tiled=True,
    )
    returned = returned.reshape(peer_count * capacity, bands * pixels)
    selector = (
        (source_rows[None, :] == jnp.arange(tile_rows, dtype=jnp.int32)[:, None]) & filled[None, :]
    ).astype(jnp.bfloat16)
    summed = jnp.dot(selector, returned, preferred_element_type=jnp.float32).reshape(
        tile_rows, bands, pixels
    )
    residual = pixel_tiles - summed
    total_sq = lax.psum(jnp.sum(residual * residual), ("grp", "dev"))
    pixel_count = float(residual.size * lax.axis_size("grp") * peer_count)
    whitened = residual / jnp.sqrt(total_sq / pixel_count + 1e-06)
    return (whitened, sed_final)


def solution(mesh):
    placed = (
        P(("grp", "dev"), None, None),
        P(("grp", "dev"), None),
        P(("grp", "dev"), None),
        P(("grp", "dev")),
        P(("grp", "dev"), None, None),
        P(("grp", "dev"), None, None, None),
    )
    return jax.shard_map(
        on_device,
        mesh=mesh,
        in_specs=placed,
        out_specs=(P(("grp", "dev"), None, None), P(("grp", "dev"), None, None)),
        check_vma=False,
    )
```

profile of v0, /device:TPU:0, one launch (start us, length us, event | category | flops | bytes accessed | tf_op | source)
XLA Modules:
  0.0 175.2 jit_solution(13595546638823699439)
XLA Ops:
  0.6 0.8 copy.28
  1.4 0.7 broadcast_multiply_fusion
  2.9 0.7 broadcast_add_fusion
  3.8 1.0 scatter_custom_fusion
  4.9 15.4 %all_to_all.19 = s32[16,1,8]{2,1,0:T(1,128)S(1)} all-to-all(s32[16,1,8]{2,1,0:T(1,128)S(1)} %bitcast.322), channel_id=1, replica_groups=mesh['grp'=2,'dev'=16] {'dev'}, dimensions={0} | all-to-all | bytes 1024 | tf_op jit(solution)/shard_map/all_to_all | solution.py:59
  20.7 3.4 %gather_fusion = bf16[128,6,512]{2,0,1:T(8,128)(2,1)S(1)} fusion(f32[64,6,512]{2,0,1:T(8,128)} %param.8, s32[1024]{0:T(1024)S(1)} %pad_clamp_fusion.1), kind=kCustom, calls=%fused_computation | custom fusion | bytes 1573376 | tf_op jit(solution)/shard_map/gather | solution.py:64
  24.1 1.1 fusion.92
  25.3 3.6 %all-to-all-start.1 = ((bf16[16,8,6,512]{3,1,2,0:T(8,128)(2,1)}), bf16[16,8,6,512]{3,1,2,0:T(8,128)(2,1)S(1)}, u32[]{:S(2)}, u32[]{:S(2)}) async-start(bf16[16,8,6,512]{3,1,2,0:T(8,128)(2,1)} %fusion.92), calls=%async_computation.1 | async-start | bytes 1572864 | tf_op jit(solution)/shard_map/all_to_all | solution.py:65
  29.2 18.2 %all-to-all-done.1 = bf16[16,8,6,512]{3,1,2,0:T(8,128)(2,1)S(1)} async-done(((bf16[16,8,6,512]{3,1,2,0:T(8,128)(2,1)}), bf16[16,8,6,512]{3,1,2,0:T(8,128)(2,1)S(1)}, u32[]{:S(2)}, u32[]{:S(2)}) %all-to-all-start.1) | async-done | bytes 786464 | tf_op jit(solution)/shard_map/all_to_all | solution.py:65
  47.7 0.6 gather_fusion.1
  48.4 54.7 %while.12 = (s32[]{:T(128)}, bf16[8,8,24,6]{2,3,1,0:T(8,128)(2,1)S(1)}, bf16[8,8,2,6,512]{4,3,2,1,0:T(8,128)(2,1)S(1)}, bf16[8,8,24,6]{2,3,1,0:T(8,128)(2,1)S(1)...) while((s32[]{:T(128)}, ...), condition=%wide.region_8.9_spmd, body=%wide.region_3.8_spmd.sunk | while | flops 44944320 | bytes 5388865 | solution.py:81
  48.5 1.6 fusion.163
  50.1 1.6 fusion.164
  51.9 1.7 fusion.166
  54.8 0.5 fusion.170
  55.4 1.6 fusion.163
  56.9 1.6 fusion.164
  58.8 1.7 fusion.166
  62.2 1.5 fusion.163
  63.8 1.5 fusion.164
  65.6 1.6 fusion.166
  68.4 0.5 fusion.170
  69.0 1.5 fusion.163
  70.6 1.5 fusion.164
  72.4 1.6 fusion.166
  75.2 0.5 fusion.170
  75.8 1.5 fusion.163
  77.4 1.5 fusion.164
  79.2 1.6 fusion.166
  82.6 1.5 fusion.163
  84.1 1.5 fusion.164
  86.0 1.6 fusion.166
  88.8 0.5 fusion.170
  89.4 1.6 fusion.163
  91.0 1.6 fusion.164
  92.8 1.7 fusion.166
  96.3 1.6 fusion.163
  97.9 1.6 fusion.164
  99.7 1.6 fusion.166
  102.6 0.5 fusion.170
  103.1 4.3 %scatter_fusion = bf16[128,6,512]{2,1,0:T(8,128)(2,1)S(1)} fusion(bf16[128,6,512]{2,1,0:T(8,128)(2,1)S(1)} %broadcast_in_dim.24, s32[128]{0:T(128)S(1)} %fusion.99, bf16[128,6,512]{2,1,0:T(8,128)(2,1)S(1)} %bitcast.319), kind=kCustom, calls=%fused_computation.3 | custom fusion | bytes 2359808 | tf_op jit(solution)/shard_map/scatter | solution.py:93
  107.5 1.2 copy.40
  108.7 4.9 %all-to-all-start.2 = ((bf16[16,8,6,512]{3,1,2,0:T(8,128)(2,1)}), bf16[16,8,6,512]{3,1,2,0:T(8,128)(2,1)S(1)}, u32[]{:S(2)}, u32[]{:S(2)}) async-start(bf16[16,8,6,512]{3,1,2,0:T(8,128)(2,1)} %copy.40), calls=%async_computation.2 | async-start | bytes 1572864 | tf_op jit(solution)/shard_map/all_to_all | solution.py:95
  113.8 0.7 copy.43
  114.5 17.6 %all-to-all-done.2 = bf16[16,8,6,512]{3,1,2,0:T(8,128)(2,1)S(1)} async-done(((bf16[16,8,6,512]{3,1,2,0:T(8,128)(2,1)}), bf16[16,8,6,512]{3,1,2,0:T(8,128)(2,1)S(1)}, u32[]{:S(2)}, u32[]{:S(2)}) %all-to-all-start.2) | async-done | bytes 786464 | tf_op jit(solution)/shard_map/all_to_all | solution.py:95
  132.5 1.0 multiply_reduce_fusion
  133.5 40.0 %psum.7 = f32[]{:T(128)} all-reduce(f32[]{:T(128)} %get-tuple-element.64), channel_id=1, replica_groups=mesh['grp'=2,'dev'=16] {'grp','dev'}, use_global_device_ids=true, to_apply=%region_11.12 | all-reduce | flops 1 | bytes 8 | tf_op jit(solution)/shard_map/psum | solution.py:110
  174.3 1.0 broadcast_divide_fusion
  (125 shorter events, 16.4 us)
Async XLA Ops:
  24.1 4.8 %copy-start.1 = (bf16[64,24,6]{0,1,2:T(8,128)(2,1)S(1)}, bf16[64,24,6]{0,1,2:T(8,128)(2,1)}, u32[]{:S(2)}) copy-start(bf16[64,24,6]{0,1,2:T(8,128)(2,1)} %param.12) | copy-start | bytes 55300
  24.1 5.0 %copy-start.2 = (s32[64]{0:T(128)S(1)}, s32[64]{0:T(128)}, u32[]{:S(2)}) copy-start(s32[64]{0:T(128)} %param.11) | copy-start | bytes 772
  25.3 22.1 %all-to-all-start.1 = ((bf16[16,8,6,512]{3,1,2,0:T(8,128)(2,1)}), bf16[16,8,6,512]{3,1,2,0:T(8,128)(2,1)S(1)}, u32[]{:S(2)}, u32[]{:S(2)}) async-start(bf16[16,8,6,512]{3,1,2,0:T(8,128)(2,1)} %fusion.92), calls=%async_computation.1 | async-start | bytes 1572864 | tf_op jit(solution)/shard_map/all_to_all | solution.py:65
  107.5 25.0 %copy-start = (f32[64,6,512]{2,0,1:T(8,128)S(1)}, f32[64,6,512]{2,0,1:T(8,128)}, u32[]{:S(2)}) copy-start(f32[64,6,512]{2,0,1:T(8,128)} %param.8) | copy-start | bytes 2359300
  108.7 23.5 %all-to-all-start.2 = ((bf16[16,8,6,512]{3,1,2,0:T(8,128)(2,1)}), bf16[16,8,6,512]{3,1,2,0:T(8,128)(2,1)S(1)}, u32[]{:S(2)}, u32[]{:S(2)}) async-start(bf16[16,8,6,512]{3,1,2,0:T(8,128)(2,1)} %copy.40), calls=%async_computation.2 | async-start | bytes 1572864 | tf_op jit(solution)/shard_map/all_to_all | solution.py:95
where the time goes:
time: 176 us; the launch traced here: 175 us
  blocking collectives  55.5 us (32%)
  matrix products  54.3 us (31%)
  waiting for transfers between devices  35.8 us (20%)
  local copies, waits for them, and re-layouts  14.3 us (8%)
  starting transfers between devices  8.54 us (5%)
  other arithmetic  4.83 us (3%)
    psum x1, blocking collectives, on_device(): total_sq = lax.psum(jnp.sum(residual * residual), ('grp', 'dev'))  40 us
    all_to_all x1, waiting for transfers between devices, on_device(): lax.all_to_all(outgoing.reshape(peer_count, capacity, bands, pixels), 'de...  18.2 us
    all_to_all x1, waiting for transfers between devices, on_device(): lax.all_to_all(outbound.reshape(peer_count, capacity, bands, pixels), 'de...  17.6 us
    all_to_all x1, blocking collectives, on_device(): lax.all_to_all(asking.reshape(peer_count, capacity), 'dev', split_axis=0,...  15.4 us
    dot_general x16, matrix products, fit_block(): jnp.einsum('nfkp,nfbp->nkb', morph, misfit, preferred_element_type=jnp.fl...  15.4 us
    dot_general x16, matrix products, fit_block(): jnp.einsum('nfkp,nfjp->nkj', morph, morph, preferred_element_type=jnp.flo...  15.2 us
    dot_general x8, matrix products, fit_block(): jnp.einsum('nkb,nfbp->nfkp', sed, misfit, preferred_element_type=jnp.floa...  13.2 us
    dot_general x16, matrix products, fit_block(): jnp.einsum('nkb,nfkp->nfbp', sed, morph, preferred_element_type=jnp.float32)  5.36 us
  transfers between devices with their start and end apart: 2, of which 2 were waited for; matrix products, arithmetic and copies ran while one was open for 1% of the time, Pallas kernels for 0%

commit v1 on v0

v1 whole, which is shorter than its diff:
```python
import functools
import math

import jax
import jax.numpy as jnp
from jax import lax
from jax.experimental import pallas as pl
from jax.experimental.pallas import tpu as pltpu
from jax.sharding import PartitionSpec as P

ITERS = 2
CHUNKS = 2
F32 = jnp.float32
BF16 = jnp.bfloat16
MESH = pl.DeviceIdType.MESH


def dot(a, b):
    return jnp.dot(a, b, preferred_element_type=F32)


def dot_nt(a, b):
    return lax.dot_general(a, b, (((1,), (1,)), ((), ())), preferred_element_type=F32)


def iota(shape, dimension):
    return lax.broadcasted_iota(jnp.int32, shape, dimension)


def split_row(shape, dimension, width):
    place = iota(shape, dimension)
    out = jnp.zeros(shape, jnp.int32)
    for cut in range(width, shape[dimension], width):
        out = out + (place >= cut).astype(jnp.int32)
    return out, place - out * width


def kernel(
    peers, regions, stride, size, tiles, source, slot, count, sed0, morph_hbm, white, sed_out,
    morph_in, mor, tgt, gram, seds, mod, pt, ptt, req, wanted, send, arrived, outb, ret, part, parts,
    in_sem, ask_s, ask_r, put_s, put_r, back_s, back_r, sum_s, sum_r,
):
    bands, tile_rows, pixels = tiles.shape
    foot, rows = source.shape
    comps = sed0.shape[1]
    groups = rows // size
    slots = peers * stride
    me = lax.axis_index("dev")
    everyone = peers * regions
    my = lax.axis_index("grp") * peers + me
    load = pltpu.make_async_copy(morph_hbm, morph_in, in_sem)
    load.start()
    barrier = pltpu.get_barrier_semaphore()

    def greet(step, carry):
        other = lax.rem(my + step, everyone)
        pl.semaphore_signal(
            barrier, inc=1, device_id={"grp": other // peers, "dev": lax.rem(other, peers)},
            device_id_type=MESH,
        )
        return carry

    lax.fori_loop(1, everyone, greet, 0)

    upper = (iota((rows, rows), 0) <= iota((rows, rows), 1)).astype(F32).astype(BF16)
    base = jnp.zeros((peers, 1), F32)
    want = jnp.zeros((slots, 1), F32)
    for f in range(foot):
        named = source[f : f + 1, :]
        hit = (iota((peers, rows), 0) == named).astype(F32)
        seen = dot(hit.astype(BF16), upper) + base
        rank = jnp.sum(hit * (seen - 1.0), axis=0, keepdims=True)
        base = base + jnp.sum(hit, axis=1, keepdims=True)
        place = named.astype(F32) * float(stride) + rank
        put = (iota((slots, rows), 0).astype(F32) == place).astype(F32)
        pt[f] = put.astype(BF16)
        ptt[f] = jnp.transpose(put).astype(BF16)
        want = want + jnp.sum(put * (slot[f : f + 1, :].astype(F32) + 1.0), axis=1, keepdims=True)
    req[...] = (
        jnp.broadcast_to(want, (slots, 128)).astype(jnp.int32).reshape(peers, stride, 128)
    )
    pl.semaphore_wait(barrier, everyone - 1)

    def exchange(src, dst, send_sem, recv_sem, lanes=None, at=None):
        def part_of(ref, index):
            return ref.at[index] if lanes is None else ref.at[index, :, lanes]

        def sem(ref, step):
            return ref.at[step] if at is None else ref.at[at, step]

        def copy(step, incoming):
            there = lax.rem(me + step, peers)
            here = lax.rem(me - step + peers, peers) if incoming else me
            return pltpu.make_async_remote_copy(
                src_ref=part_of(src, there), dst_ref=part_of(dst, here),
                send_sem=sem(send_sem, step), recv_sem=sem(recv_sem, step),
                device_id={"dev": there}, device_id_type=MESH,
            )

        def start():
            def body(step, carry):
                copy(step, False).start()
                return carry

            lax.fori_loop(1, peers, body, 0)

        def wait_in():
            def body(step, carry):
                copy(step, True).wait_recv()
                return carry

            lax.fori_loop(1, peers, body, 0)

        def wait_out():
            def body(step, carry):
                copy(step, False).wait_send()
                return carry

            lax.fori_loop(1, peers, body, 0)

        return start, wait_in, wait_out

    ask, ask_in, ask_out = exchange(req, wanted, ask_s, ask_r)
    ask()
    wanted[me] = req[me]

    width = size * comps
    span = size * bands
    blend_row, comp_row = split_row((width, 1), 0, comps)
    blend_col, _ = split_row((1, width), 1, comps)
    band_col, member_col = split_row((1, span), 1, size)
    same = (blend_row == blend_col).astype(F32)
    same_bd = (blend_row == member_col).astype(F32)
    spread = (iota((width, comps), 1) == comp_row).astype(F32).astype(BF16)
    gather_k = (
        iota((comps, width), 0) == split_row((1, width), 1, comps)[1]
    ).astype(F32).astype(BF16)
    sed_all = jnp.concatenate([sed0[b].astype(F32) for b in range(bands)], axis=1).astype(BF16)
    band_of, blend_of = split_row((bands * rows, 1), 0, rows)

    def chosen(g):
        return (
            ((band_of == band_col) & (blend_of == g * size + member_col)).astype(F32)
        )

    load.wait()

    def begin(g, carry):
        held = jnp.sum(
            jnp.where(iota((width, rows), 1) == g * size + blend_row, count[...], 0).astype(F32),
            axis=1, keepdims=True,
        )
        active = (comp_row.astype(F32) < held).astype(F32)
        first = dot(sed_all, chosen(g).astype(BF16))
        seds[g] = dot(spread, first.astype(BF16)) * same_bd * active
        total = jnp.zeros((width, width), F32)
        for f in range(foot):
            whole = morph_in[pl.ds(g * size, size), f].astype(F32).reshape(width, pixels)
            masked = (whole * active).astype(BF16)
            mor[g, f] = masked
        return carry

    lax.fori_loop(0, groups, begin, 0)
    ask_in()
    picks = (wanted[...].reshape(slots, 128)[:, :tile_rows] - 1 == iota((slots, tile_rows), 1)).astype(F32)
    pick = picks.astype(BF16)
    for b in range(bands):
        block = dot(pick, tiles[b].astype(BF16)).astype(BF16).astype(F32)
        send[:, :, b * pixels : (b + 1) * pixels] = block.reshape(peers, stride, pixels).astype(BF16)
    fetch, fetch_in, fetch_out = exchange(send, arrived, put_s, put_r)
    fetch()
    arrived[me] = send[me]

    def first_gram(g, carry):
        total = dot_nt(mor[g, 0], mor[g, 0])
        for f in range(1, foot):
            total = total + dot_nt(mor[g, f], mor[g, f])
        gram[g] = total * same
        return carry

    lax.fori_loop(0, groups, first_gram, 0)
    fetch_in()
    for b in range(bands):
        block = arrived[:, :, b * pixels : (b + 1) * pixels].astype(F32)
        block = block.reshape(slots, pixels).astype(BF16)
        for f in range(foot):
            tgt[:, f, b * size : (b + 1) * size, :] = dot(ptt[f], block).reshape(
                groups, size, pixels
            )

    def norm(square, mask):
        flat = jnp.sum(square, axis=0, keepdims=True)
        return jnp.sqrt(jnp.sum(mask * flat, axis=1, keepdims=True)) + 1.0

    def fit(g, placed):
        sed = seds[g]
        for sweep in range(ITERS):
            if sweep == 0:
                grams = gram[g]
            else:
                grams = dot_nt(mor[g, 0], mor[g, 0])
                for f in range(1, foot):
                    grams = grams + dot_nt(mor[g, f], mor[g, f])
                grams = grams * same
            cross = dot_nt(mor[g, 0], tgt[g, 0].astype(BF16))
            for f in range(1, foot):
                cross = cross + dot_nt(mor[g, f], tgt[g, f].astype(BF16))
            step = 1.0 / norm(grams * grams, same)
            slope = dot(grams.astype(BF16), sed.astype(BF16)) - cross * same_bd
            sed = jnp.maximum(sed - slope * step, 0.0).astype(BF16).astype(F32)
            sed_b = sed.astype(BF16)
            sed_t = jnp.transpose(sed).astype(BF16)
            small = dot(sed_t, sed_b)
            step = 1.0 / norm(small * small, same_bd)
            for f in range(foot):
                misfit = (dot(sed_t, mor[g, f]) - tgt[g, f]).astype(BF16)
                slope = dot(sed_b, misfit)
                mor[g, f] = jnp.maximum(
                    mor[g, f].astype(F32) - (slope + 0.1) * step, 0.0
                ).astype(BF16)
        for f in range(foot):
            mod[f, :, pl.ds(pl.multiple_of(g * size, size), size), :] = dot(
                sed_t, mor[g, f]
            ).reshape(bands, size, pixels)
        lean = dot(gather_k, sed_b)
        return placed + dot_nt(lean.astype(BF16), chosen(g).astype(BF16))

    placed = lax.fori_loop(0, groups, fit, jnp.zeros((comps, bands * rows), F32))
    for b in range(bands):
        sed_out[b] = placed[:, b * rows : (b + 1) * rows].astype(BF16)

    each = bands // CHUNKS
    trips = []
    for chunk in range(CHUNKS):
        for b in range(chunk * each, (chunk + 1) * each):
            block = dot(pt[0], mod[0, b].astype(BF16))
            for f in range(1, foot):
                block = block + dot(pt[f], mod[f, b].astype(BF16))
            outb[:, :, b * pixels : (b + 1) * pixels] = block.reshape(
                peers, stride, pixels
            ).astype(BF16)
        lanes = slice(chunk * each * pixels, (chunk + 1) * each * pixels)
        trips.append(exchange(outb, ret, back_s, back_r, lanes, chunk))
        trips[-1][0]()
    ret[me] = outb[me]
    pick_t = jnp.transpose(picks).astype(BF16)
    squares = jnp.zeros((8, 128), F32)
    for chunk in range(CHUNKS):
        trips[chunk][1]()
        for b in range(chunk * each, (chunk + 1) * each):
            block = ret[:, :, b * pixels : (b + 1) * pixels].astype(F32)
            block = block.reshape(slots, pixels).astype(BF16)
            residual = tiles[b] - dot(pick_t, block)
            white[b] = residual
            square = residual * residual
            for r in range(0, tile_rows, 8):
                for c in range(0, pixels, 128):
                    squares = squares + square[r : r + 8, c : c + 128]

    part[...] = squares

    def share(step, incoming):
        there = lax.rem(my + step, everyone)
        here = lax.rem(my - step + everyone, everyone) if incoming else my
        return pltpu.make_async_remote_copy(
            src_ref=part, dst_ref=parts.at[here], send_sem=sum_s.at[step],
            recv_sem=sum_r.at[step],
            device_id={"grp": there // peers, "dev": lax.rem(there, peers)}, device_id_type=MESH,
        )

    def start_share(step, carry):
        share(step, False).start()
        return carry

    def end_share(step, carry):
        share(step, True).wait_recv()
        return carry

    def end_sent(step, carry):
        share(step, False).wait_send()
        return carry

    lax.fori_loop(1, everyone, start_share, 0)
    parts[my] = squares
    ask_out()
    fetch_out()
    for trip in trips:
        trip[2]()
    lax.fori_loop(1, everyone, end_share, 0)
    total = jnp.sum(parts[...], axis=0)
    total = jnp.sum(jnp.sum(total, axis=1, keepdims=True), axis=0, keepdims=True)
    count_all = float(bands * tile_rows * pixels * everyone)
    scale = 1.0 / jnp.sqrt(total / count_all + 1e-06)
    for b in range(bands):
        white[b] = white[b] * scale
    lax.fori_loop(1, everyone, end_sent, 0)


def on_device(pixel_tiles, blend_source, blend_slot, component_count, sed_start, morph_start):
    peers = lax.axis_size("dev")
    regions = lax.axis_size("grp")
    rows, foot = blend_source.shape
    tile_rows, bands, pixels = pixel_tiles.shape
    comps = sed_start.shape[1]
    entries = rows * foot
    capacity = max(2, (entries + peers - 1) // peers)
    stride = (capacity + 7) // 8 * 8
    size = math.gcd(rows, 8)
    groups = rows // size
    slots = peers * stride
    flat = bands * pixels
    vmem = pl.BlockSpec(memory_space=pltpu.VMEM)
    dma = pltpu.SemaphoreType.DMA
    white, sed_final = pl.pallas_call(
        functools.partial(kernel, peers, regions, stride, size),
        out_shape=(
            jax.ShapeDtypeStruct((bands, tile_rows, pixels), F32),
            jax.ShapeDtypeStruct((bands, comps, rows), BF16),
        ),
        in_specs=[vmem] * 5 + [pl.BlockSpec(memory_space=pl.ANY)],
        out_specs=(vmem, vmem),
        scratch_shapes=[
            pltpu.VMEM(morph_start.shape, BF16),
            pltpu.VMEM((groups, foot, size * comps, pixels), BF16),
            pltpu.VMEM((groups, foot, size * bands, pixels), F32),
            pltpu.VMEM((groups, size * comps, size * comps), F32),
            pltpu.VMEM((groups, size * comps, size * bands), F32),
            pltpu.VMEM((foot, bands, rows, pixels), F32),
            pltpu.VMEM((foot, slots, rows), BF16),
            pltpu.VMEM((foot, rows, slots), BF16),
            pltpu.VMEM((peers, stride, 128), jnp.int32),
            pltpu.VMEM((peers, stride, 128), jnp.int32),
            pltpu.VMEM((peers, stride, flat), BF16),
            pltpu.VMEM((peers, stride, flat), BF16),
            pltpu.VMEM((peers, stride, flat), BF16),
            pltpu.VMEM((peers, stride, flat), BF16),
            pltpu.VMEM((8, 128), F32),
            pltpu.VMEM((peers * regions, 8, 128), F32),
            dma,
            dma((peers,)),
            dma((peers,)),
            dma((peers,)),
            dma((peers,)),
            dma((CHUNKS, peers)),
            dma((CHUNKS, peers)),
            dma((peers * regions,)),
            dma((peers * regions,)),
        ],
        compiler_params=pltpu.CompilerParams(
            collective_id=0, has_side_effects=True, vmem_limit_bytes=60 * 1024 * 1024
        ),
    )(
        jnp.transpose(pixel_tiles, (1, 0, 2)),
        jnp.transpose(blend_source),
        jnp.transpose(blend_slot),
        component_count.reshape(1, rows),
        jnp.transpose(sed_start, (2, 1, 0)),
        morph_start,
    )
    return jnp.transpose(white, (1, 0, 2)), jnp.transpose(sed_final, (2, 1, 0))


def solution(mesh):
    placed = (
        P(("grp", "dev"), None, None),
        P(("grp", "dev"), None),
        P(("grp", "dev"), None),
        P(("grp", "dev")),
        P(("grp", "dev"), None, None),
        P(("grp", "dev"), None, None, None),
    )
    return jax.shard_map(
        on_device,
        mesh=mesh,
        in_specs=placed,
        out_specs=(P(("grp", "dev"), None, None), P(("grp", "dev"), None, None)),
        check_vma=False,
    )
```

time: 176 us -> 79.5 us (0.45)
  Pallas kernels: 0 us -> 75.1 us
  blocking collectives: 55.5 us -> 0 us
  matrix products: 54.3 us -> 0 us
  waiting for transfers between devices: 35.8 us -> 0 us
  local copies, waits for them, and re-layouts: 14.3 us -> 3.48 us
  starting transfers between devices: 8.54 us -> 0 us
  other arithmetic: 4.83 us -> 0 us
    pallas_call x0 -> x1, Pallas kernels: none -> 75.1 us  [on_device(): pl.pallas_call(functools.partial(kernel, peers, regions, stride, size), o...]
    dot_general x73 -> x0, matrix products: 54.3 us -> none  [the longest x16 15.4 us: fit_block(): jnp.einsum('nfkp,nfbp->nkb', morph, misfit, preferred_element_type=jnp.fl...]
    psum x1 -> x0, blocking collectives: 40 us -> none  [on_device(): total_sq = lax.psum(jnp.sum(residual * residual), ('grp', 'dev'))]
    all_to_all x2 -> x0, waiting for transfers between devices: 35.8 us -> none  [the longest x1 18.2 us: on_device(): lax.all_to_all(outgoing.reshape(peer_count, capacity, bands, pixels), 'de...]
    all_to_all x1 -> x0, blocking collectives: 15.4 us -> none  [on_device(): lax.all_to_all(asking.reshape(peer_count, capacity), 'dev', split_axis=0,...]
    all_to_all x2 -> x0, starting transfers between devices: 8.54 us -> none  [the longest x1 4.92 us: on_device(): lax.all_to_all(outbound.reshape(peer_count, capacity, bands, pixels), 'de...]
    scatter x2 -> x0, local copies, waits for them, and re-layouts: 5.31 us -> none  [the longest x1 4.33 us: on_device(): jnp.zeros((peer_count * capacity, bands, pixels), jnp.bfloat16).at[placing]]
    gather x2 -> x0, local copies, waits for them, and re-layouts: 4.07 us -> none  [the longest x1 3.42 us: on_device(): pixel_tiles[source_rows]]
  transfers between devices with their start and end apart: 2 -> 0, of which waited for: 2 -> 0; matrix products, arithmetic and copies ran while one was open for 1% -> 0% of each run, Pallas kernels for 0% -> 0%
where the time goes in v1:
time: 79.5 us; the launch traced here: 79.2 us
  Pallas kernels  75.1 us (94%)
  local copies, waits for them, and re-layouts  3.48 us (4%)
    pallas_call x1, Pallas kernels, on_device(): pl.pallas_call(functools.partial(kernel, peers, regions, stride, size), o...  75.1 us
    unnamed x2, local copies, waits for them, and re-layouts  3.48 us

profile of v1, /device:TPU:0, one launch (start us, length us, event | category | flops | bytes accessed | tf_op | source)
XLA Modules:
  0.0 79.2 jit_solution(5660991528007064132)
XLA Ops:
  0.6 75.1 %shard_map.77 = (f32[6,64,512]{2,1,0:T(8,128)}, bf16[6,24,64]{2,1,0:T(8,128)(2,1)}) custom-call(f32[6,64,512]{2,1,0:T(8,128)} %bitcast.8, s32[2,64]{1,0:T(2,128)} %bitcast.11, s32[2,64]{1,0:T(2,128)} %bitcast.12, s32[1,64]{1,0:T(1,128)} %bitcast.13, bf16[6,24,64]{2,1,0:T(8,128)(2,1)} %bitcast.9, bf16[64,2,24,512]{3,2,1,0:T(8,128)(2,1)} %morph_hbm.1), custom_call_target="tpu_custom_call" | custom-call | tf_op jit(solution)/shard_map/pallas_call | solution.py:314
  75.7 2.1 %copy.10 = f32[64,6,512]{2,0,1:T(8,128)} copy(f32[64,6,512]{2,0,1:T(8,128)} %bitcast.7) | data formatting | bytes 1572864
  77.8 1.4 %copy.11 = bf16[64,24,6]{0,1,2:T(8,128)(2,1)} copy(bf16[64,24,6]{0,1,2:T(8,128)(2,1)} %bitcast.10) | data formatting | bytes 36864

commit v2 on v1

v2 whole, which is shorter than its diff:
```python
import functools
import math

import jax
import jax.numpy as jnp
from jax import lax
from jax.experimental import pallas as pl
from jax.experimental.pallas import tpu as pltpu
from jax.sharding import PartitionSpec as P

INWARD = 1
OUTWARD = 2
F32 = jnp.float32
BF16 = jnp.bfloat16
MESH = pl.DeviceIdType.MESH


def dot(a, b):
    return jnp.dot(a, b, preferred_element_type=F32)


def dot_nt(a, b):
    return lax.dot_general(a, b, (((1,), (1,)), ((), ())), preferred_element_type=F32)


def iota(shape, dimension):
    return lax.broadcasted_iota(jnp.int32, shape, dimension)


def split_row(shape, dimension, width):
    place = iota(shape, dimension)
    out = jnp.zeros(shape, jnp.int32)
    for cut in range(width, shape[dimension], width):
        out = out + (place >= cut).astype(jnp.int32)
    return out, place - out * width


def kernel(
    peers, regions, stride, size, tiles, source, slot, count, sed0, morph_hbm, white, sed_out, scale_out,
    morph_in, mor, tgt, mis, gram, seds, sed_b, sed_step, morph_step, mod, pt, ptt, req, wanted, send, arrived, outb, ret, part, parts,
    in_sem, ask_s, ask_r, put_s, put_r, back_s, back_r, sum_s, sum_r,
):
    bands, tile_rows, pixels = tiles.shape
    foot, rows = source.shape
    comps = sed0.shape[1]
    groups = rows // size
    slots = peers * stride
    me = lax.axis_index("dev")
    everyone = peers * regions
    my = lax.axis_index("grp") * peers + me
    load = pltpu.make_async_copy(morph_hbm, morph_in, in_sem)
    load.start()
    barrier = pltpu.get_barrier_semaphore()

    def greet(step, carry):
        other = lax.rem(my + step, everyone)
        pl.semaphore_signal(
            barrier, inc=1, device_id={"grp": lax.div(other, peers), "dev": lax.rem(other, peers)},
            device_id_type=MESH,
        )
        return carry

    lax.fori_loop(1, everyone, greet, 0)

    upper = (iota((rows, rows), 0) <= iota((rows, rows), 1)).astype(F32).astype(BF16)
    base = jnp.zeros((peers, 1), F32)
    want = jnp.zeros((slots, 1), F32)
    for f in range(foot):
        named = source[f : f + 1, :]
        hit = (iota((peers, rows), 0) == named).astype(F32)
        seen = dot(hit.astype(BF16), upper) + base
        rank = jnp.sum(hit * (seen - 1.0), axis=0, keepdims=True)
        base = base + jnp.sum(hit, axis=1, keepdims=True)
        place = named.astype(F32) * float(stride) + rank
        put = (iota((slots, rows), 0).astype(F32) == place).astype(F32)
        pt[f] = put.astype(BF16)
        ptt[f] = jnp.transpose(put).astype(BF16)
        want = want + jnp.sum(put * (slot[f : f + 1, :].astype(F32) + 1.0), axis=1, keepdims=True)
    req[...] = (
        jnp.broadcast_to(want, (slots, 128)).astype(jnp.int32).reshape(peers, stride, 128)
    )
    pl.semaphore_wait(barrier, everyone - 1)

    def exchange(src, dst, send_sem, recv_sem, lanes=None, at=None):
        def part_of(ref, index):
            return ref.at[index] if lanes is None else ref.at[index, :, lanes]

        def sem(ref, step):
            return ref.at[step] if at is None else ref.at[at, step]

        def copy(step, incoming):
            there = lax.rem(me + step, peers)
            here = lax.rem(me - step + peers, peers) if incoming else me
            return pltpu.make_async_remote_copy(
                src_ref=part_of(src, there), dst_ref=part_of(dst, here),
                send_sem=sem(send_sem, step), recv_sem=sem(recv_sem, step),
                device_id={"dev": there}, device_id_type=MESH,
            )

        def start():
            def body(step, carry):
                copy(step, False).start()
                return carry

            lax.fori_loop(1, peers, body, 0)

        def wait_in():
            def body(step, carry):
                copy(step, True).wait_recv()
                return carry

            lax.fori_loop(1, peers, body, 0)

        def wait_out():
            def body(step, carry):
                copy(step, False).wait_send()
                return carry

            lax.fori_loop(1, peers, body, 0)

        return start, wait_in, wait_out

    ask, ask_in, ask_out = exchange(req, wanted, ask_s, ask_r)
    ask()
    wanted[me] = req[me]

    width = size * comps
    span = size * bands
    blend_row, comp_row = split_row((width, 1), 0, comps)
    blend_col, comp_col = split_row((1, width), 1, comps)
    _, member_col = split_row((1, span), 1, size)
    band_row, member_row = split_row((span, 1), 0, size)
    same = (blend_row == blend_col).astype(F32)
    same_bd = (blend_row == member_col).astype(F32)
    same_t = (member_row == blend_col).astype(F32)
    gather_k = (iota((comps, width), 0) == comp_col).astype(F32).astype(BF16)
    sed_all = jnp.concatenate([sed0[b].astype(F32) for b in range(bands)], axis=1).astype(BF16)
    band_of, blend_of = split_row((1, bands * rows), 1, rows)
    counts = jnp.broadcast_to(count[...], (8, rows)).astype(F32).astype(BF16)
    pair = 2 if groups % 2 == 0 else 1

    def chosen(g):
        hit = (band_of == band_row) & (blend_of == g * size + member_row)
        return hit.astype(F32).astype(BF16)

    def norm(square, mask):
        flat = jnp.sum(square, axis=0, keepdims=True)
        return jnp.sqrt(jnp.sum(mask * flat, axis=1, keepdims=True)) + 1.0

    def wide(column):
        return jnp.broadcast_to(column, (column.shape[0], 128))

    def over_groups(body, pair=pair):
        def both(j, carry):
            stores = []
            for k in range(pair):
                stores = stores + body(j * pair + k)
            for ref, index, value in stores:
                ref[index] = value
            return carry

        lax.fori_loop(0, groups // pair, both, 0)

    load.wait()

    def begin(g):
        held = jnp.sum(
            jnp.where(iota((width, rows), 1) == g * size + blend_row, count[...], 0).astype(F32),
            axis=1, keepdims=True,
        )
        active = (comp_row.astype(F32) < held).astype(F32)
        owner = (iota((rows, width), 0) == g * size + blend_col).astype(F32).astype(BF16)
        active_t = (comp_col.astype(F32) < dot(counts, owner)[0:1]).astype(F32)
        first = dot_nt(chosen(g), sed_all)
        stores = [(seds, g, dot(first.astype(BF16), gather_k) * same_t * active_t)]
        for f in range(foot):
            whole = morph_in[pl.ds(g * size, size), f].astype(F32).reshape(width, pixels)
            stores.append((mor, (g, f), (whole * active).astype(BF16)))
        return stores

    over_groups(begin)
    ask_in()
    picks = (wanted[...].reshape(slots, 128)[:, :tile_rows] - 1 == iota((slots, tile_rows), 1)).astype(F32)
    pick = picks.astype(BF16)
    arrivals = INWARD if bands % INWARD == 0 else 1
    each = bands // arrivals
    fetches = []
    for c in range(arrivals):
        for b in range(c * each, (c + 1) * each):
            block = dot(pick, tiles[b].astype(BF16))
            send[:, :, b * pixels : (b + 1) * pixels] = block.reshape(
                peers, stride, pixels
            ).astype(BF16)
        lanes = slice(c * each * pixels, (c + 1) * each * pixels)
        fetches.append(exchange(send, arrived, put_s, put_r, lanes, c))
        fetches[-1][0]()
    arrived[me] = send[me]

    def grams_of(morphs):
        total = dot_nt(morphs[0], morphs[0])
        for f in range(1, foot):
            total = total + dot_nt(morphs[f], morphs[f])
        return total * same

    def cross_of(targets, morphs):
        total = dot_nt(targets[0], morphs[0])
        for f in range(1, foot):
            total = total + dot_nt(targets[f], morphs[f])
        return total

    def first_gram(g):
        total = grams_of([mor[g, f] for f in range(foot)])
        step = 1.0 / norm(total * total, same_t)
        return [(gram, g, total.astype(BF16)), (sed_step, g, wide(step))]

    over_groups(first_gram)

    for c in range(arrivals):
        fetches[c][1]()
        for b in range(c * each, (c + 1) * each):
            block = arrived[:, :, b * pixels : (b + 1) * pixels].astype(F32)
            block = block.reshape(slots, pixels).astype(BF16)
            for f in range(foot):
                tgt[:, f, b * size : (b + 1) * size, :] = dot(ptt[f], block).reshape(
                    groups, size, pixels
                )
        part_rows = slice(c * each * size, (c + 1) * each * size)

        def first_seds(g):
            targets = [tgt[g, f, part_rows] for f in range(foot)]
            morphs = [mor[g, f] for f in range(foot)]
            cross = cross_of([t.astype(BF16) for t in targets], morphs) * same_t[part_rows]
            old = seds[g, part_rows]
            slope = dot(old.astype(BF16), gram[g]) - cross
            sed = jnp.maximum(old - slope * sed_step[g, part_rows, 0:1], 0.0).astype(BF16)
            stores = [(seds, (g, part_rows), sed.astype(F32))]
            for f in range(foot):
                misfit = (dot(sed, morphs[f]) - targets[f]).astype(BF16)
                stores.append((mis, (g, f, part_rows), misfit))
            return stores

        over_groups(first_seds)

    def moved(morph, slope, step):
        return jnp.maximum(morph.astype(F32) - (slope + 0.1) * step, 0.0).astype(BF16)

    def morph_stepsize(sed):
        small = dot_nt(sed, sed)
        return 1.0 / norm(small * small, same_bd)

    def second_seds(g):
        old = seds[g]
        step = morph_stepsize(old.astype(BF16))
        lhs = jnp.transpose(old).astype(BF16)
        morphs = [moved(mor[g, f], dot(lhs, mis[g, f]), step) for f in range(foot)]
        stores = [(mor, (g, f), morphs[f]) for f in range(foot)]
        total = grams_of(morphs)
        cross = cross_of([tgt[g, f].astype(BF16) for f in range(foot)], morphs) * same_t
        slope = dot(old.astype(BF16), total.astype(BF16)) - cross
        sed = jnp.maximum(old - slope / norm(total * total, same_t), 0.0).astype(BF16)
        stores.append((seds, g, sed.astype(F32)))
        stores.append((sed_b, g, jnp.transpose(sed.astype(F32)).astype(BF16)))
        stores.append((morph_step, g, wide(morph_stepsize(sed))))
        return stores

    over_groups(second_seds)

    window = pixels // OUTWARD
    trips = []
    for chunk in range(OUTWARD):
        taken = slice(chunk * window, (chunk + 1) * window)

        def last_models(g):
            sed = seds[g].astype(BF16)
            stores = []
            for f in range(foot):
                morph = mor[g, f, :, taken]
                misfit = (dot(sed, morph) - tgt[g, f, :, taken]).astype(BF16)
                morph = moved(morph, dot(sed_b[g], misfit), morph_step[g, :, 0:1])
                model = dot(sed, morph).reshape(bands, size, window)
                member = pl.ds(pl.multiple_of(g * size, size), size)
                stores.append((mod, (f, slice(None), member, slice(None)), model))
            return stores

        over_groups(last_models)
        for b in range(bands):
            block = dot(pt[0], mod[0, b].astype(BF16))
            for f in range(1, foot):
                block = block + dot(pt[f], mod[f, b].astype(BF16))
            at = (chunk * bands + b) * window
            outb[:, :, at : at + window] = block.reshape(peers, stride, window).astype(BF16)
        lanes = slice(chunk * bands * window, (chunk + 1) * bands * window)
        trips.append(exchange(outb, ret, back_s, back_r, lanes, chunk))
        trips[-1][0]()
    ret[me] = outb[me]

    def place(g, placed):
        lean = dot_nt(gather_k, seds[g].astype(BF16))
        return placed + dot(lean.astype(BF16), chosen(g))

    placed = lax.fori_loop(0, groups, place, jnp.zeros((comps, bands * rows), F32))
    for b in range(bands):
        sed_out[b] = placed[:, b * rows : (b + 1) * rows].astype(BF16)
    pick_t = jnp.transpose(picks).astype(BF16)
    squares = jnp.zeros((8, 128), F32)
    for chunk in range(OUTWARD):
        trips[chunk][1]()
        taken = slice(chunk * window, (chunk + 1) * window)
        for b in range(bands):
            at = (chunk * bands + b) * window
            block = ret[:, :, at : at + window].astype(F32).reshape(slots, window).astype(BF16)
            residual = tiles[b, :, taken] - dot(pick_t, block)
            white[b, :, taken] = residual
            square = residual * residual
            for r in range(0, tile_rows, 8):
                for c in range(0, window, 128):
                    squares = squares + square[r : r + 8, c : c + 128]

    own_row = jnp.sum(squares, axis=0, keepdims=True)
    part[...] = own_row

    def share(step, incoming):
        there = lax.rem(my + step, everyone)
        here = lax.rem(my - step + everyone, everyone) if incoming else my
        return pltpu.make_async_remote_copy(
            src_ref=part, dst_ref=parts.at[here], send_sem=sum_s.at[step],
            recv_sem=sum_r.at[step],
            device_id={"grp": lax.div(there, peers), "dev": lax.rem(there, peers)}, device_id_type=MESH,
        )

    def start_share(step, carry):
        share(step, False).start()
        return carry

    def end_share(step, carry):
        share(step, True).wait_recv()
        return carry

    def end_sent(step, carry):
        share(step, False).wait_send()
        return carry

    lax.fori_loop(1, everyone, start_share, 0)
    parts[my] = own_row
    ask_out()
    for trip in fetches + trips:
        trip[2]()
    lax.fori_loop(1, everyone, end_share, 0)
    total = jnp.sum(parts[...], axis=0)
    total = jnp.sum(jnp.sum(total, axis=1, keepdims=True), axis=0, keepdims=True)
    count_all = float(bands * tile_rows * pixels * everyone)
    scale_out[...] = jnp.broadcast_to(1.0 / jnp.sqrt(total / count_all + 1e-06), (8, 128))
    lax.fori_loop(1, everyone, end_sent, 0)


def on_device(pixel_tiles, blend_source, blend_slot, component_count, sed_start, morph_start):
    peers = lax.axis_size("dev")
    regions = lax.axis_size("grp")
    rows, foot = blend_source.shape
    tile_rows, bands, pixels = pixel_tiles.shape
    comps = sed_start.shape[1]
    entries = rows * foot
    capacity = max(2, (entries + peers - 1) // peers)
    stride = (capacity + 7) // 8 * 8
    size = math.gcd(rows, 8)
    groups = rows // size
    slots = peers * stride
    flat = bands * pixels
    vmem = pl.BlockSpec(memory_space=pltpu.VMEM)
    dma = pltpu.SemaphoreType.DMA
    residual, sed_final, scale = pl.pallas_call(
        functools.partial(kernel, peers, regions, stride, size),
        out_shape=(
            jax.ShapeDtypeStruct((bands, tile_rows, pixels), F32),
            jax.ShapeDtypeStruct((bands, comps, rows), BF16),
            jax.ShapeDtypeStruct((8, 128), F32),
        ),
        in_specs=[vmem] * 5 + [pl.BlockSpec(memory_space=pl.ANY)],
        out_specs=(vmem, vmem, vmem),
        scratch_shapes=[
            pltpu.VMEM(morph_start.shape, BF16),
            pltpu.VMEM((groups, foot, size * comps, pixels), BF16),
            pltpu.VMEM((groups, foot, size * bands, pixels), F32),
            pltpu.VMEM((groups, foot, size * bands, pixels), BF16),
            pltpu.VMEM((groups, size * comps, size * comps), BF16),
            pltpu.VMEM((groups, size * bands, size * comps), F32),
            pltpu.VMEM((groups, size * comps, size * bands), BF16),
            pltpu.VMEM((groups, size * bands, 128), F32),
            pltpu.VMEM((groups, size * comps, 128), F32),
            pltpu.VMEM((foot, bands, rows, pixels // OUTWARD), F32),
            pltpu.VMEM((foot, slots, rows), BF16),
            pltpu.VMEM((foot, rows, slots), BF16),
            pltpu.VMEM((peers, stride, 128), jnp.int32),
            pltpu.VMEM((peers, stride, 128), jnp.int32),
            pltpu.VMEM((peers, stride, flat), BF16),
            pltpu.VMEM((peers, stride, flat), BF16),
            pltpu.VMEM((peers, stride, flat), BF16),
            pltpu.VMEM((peers, stride, flat), BF16),
            pltpu.VMEM((1, 128), F32),
            pltpu.VMEM((peers * regions, 1, 128), F32),
            dma,
            dma((peers,)),
            dma((peers,)),
            dma((INWARD, peers)),
            dma((INWARD, peers)),
            dma((OUTWARD, peers)),
            dma((OUTWARD, peers)),
            dma((peers * regions,)),
            dma((peers * regions,)),
        ],
        compiler_params=pltpu.CompilerParams(
            collective_id=0, has_side_effects=True, vmem_limit_bytes=60 * 1024 * 1024
        ),
    )(
        jnp.transpose(pixel_tiles, (1, 0, 2)),
        jnp.transpose(blend_source),
        jnp.transpose(blend_slot),
        component_count.reshape(1, rows),
        jnp.transpose(sed_start, (2, 1, 0)),
        morph_start,
    )
    white = residual * scale[0, 0]
    return jnp.transpose(white, (1, 0, 2)), jnp.transpose(sed_final, (2, 1, 0))


def solution(mesh):
    placed = (
        P(("grp", "dev"), None, None),
        P(("grp", "dev"), None),
        P(("grp", "dev"), None),
        P(("grp", "dev")),
        P(("grp", "dev"), None, None),
        P(("grp", "dev"), None, None, None),
    )
    return jax.shard_map(
        on_device,
        mesh=mesh,
        in_specs=placed,
        out_specs=(P(("grp", "dev"), None, None), P(("grp", "dev"), None, None)),
        check_vma=False,
    )
```

time: 79.5 us -> 77.8 us (0.979)
  Pallas kernels: 75.1 us -> 71.6 us
  other arithmetic: 0 us -> 2.75 us
  local copies, waits for them, and re-layouts: 3.48 us -> 2.57 us
    pallas_call x1, Pallas kernels: 75.1 us -> 71.6 us  [on_device(): pl.pallas_call(functools.partial(kernel, peers, regions, stride, size), o...]
    transpose x0 -> x1, other arithmetic: none -> 2.75 us  [on_device(): jnp.transpose(white, (1, 0, 2))]
    unnamed x2 -> x1, local copies, waits for them, and re-layouts: 3.48 us -> 1.39 us
    slice x0 -> x1, local copies, waits for them, and re-layouts: none -> 1.19 us  [on_device(): white = residual * scale[0, 0]]
where the time goes in v2:
time: 77.8 us; the launch traced here: 77.5 us
  Pallas kernels  71.6 us (92%)
  other arithmetic  2.75 us (4%)
  local copies, waits for them, and re-layouts  2.57 us (3%)
    pallas_call x1, Pallas kernels, on_device(): pl.pallas_call(functools.partial(kernel, peers, regions, stride, size), o...  71.6 us
    transpose x1, other arithmetic, on_device(): jnp.transpose(white, (1, 0, 2))  2.75 us

profile of v2, /device:TPU:0, one launch (start us, length us, event | category | flops | bytes accessed | tf_op | source)
XLA Modules:
  0.0 77.5 jit_solution(7134839931560537624)
XLA Ops:
  0.6 71.6 %shard_map.77 = (f32[6,64,512]{2,1,0:T(8,128)}, bf16[6,24,64]{2,1,0:T(8,128)(2,1)}, f32[8,128]{1,0:T(8,128)}) custom-call(f32[6,64,512]{2,1,0:T(8,128)} %bitcast.9, s32[2,64]{1,0:T(2,128)} %bitcast.12, s32[2,64]{1,0:T(2,128)} %bitcast.13, s32[1,64]{1,0:T(1,128)} %bitcast.14, bf16[6,24,64]{2,1,0:T(8,128)(2,1)} %bitcast.10, bf16[64,2,24,512]{3,2,1,0:T(8,128)(2,1)} %morph_hbm.1), custom_call_target="tpu_custom_call" | custom-call | tf_op jit(solution)/shard_map/pallas_call | solution.py:371
  72.2 1.2 %slice.3 = f32[1,1]{1,0:T(1,128)} slice(f32[8,128]{1,0:T(8,128)} %get-tuple-element.6), slice={[0:1], [0:1]} | slice | bytes 8 | tf_op jit(solution)/shard_map/slice | solution.py:422
  73.4 2.7 %multiply_bitcast_fusion = f32[64,6,512]{2,0,1:T(8,128)} fusion(f32[6,64,512]{2,1,0:T(8,128)} %get-tuple-element.5, f32[]{:T(128)} %bitcast.5), kind=kLoop, calls=%fused_computation | loop fusion | flops 196608 | bytes 1572868 | tf_op jit(solution)/shard_map/transpose | solution.py:423
  76.1 1.4 %copy.9 = bf16[64,24,6]{0,1,2:T(8,128)(2,1)} copy(bf16[64,24,6]{0,1,2:T(8,128)(2,1)} %bitcast.11) | data formatting | bytes 36864
